TPU v7x, 32 devices: a whole 2x2x4 slice. The times are simulated.
32 devices in a mesh: gx: 4 (over z), gy: 8 (over y, x, core).
Axes of the slice: x: 2, y: 2, z: 4, core: 2. Of those that a mesh axis runs over, the one named last changes fastest.
Arguments:
- stored_vectors: bfloat16 [2, 16, 32, 4096], P(None, None, 'gx', 'gy'), may hold values from -4 to 4
- disorder: float32 [2, 32, 4096], P(None, 'gx', 'gy'), may hold values from -1.5 to 1.5
- vacancy: int32 [2, 32, 4096], P(None, 'gx', 'gy'), may hold values 0 or 1
- plan: int32 [32], replicated, may hold values from 0 to 31, as said below
Outputs:
- local_moments: float32 [4, 2, 32, 4096], P(None, None, 'gx', 'gy')
- trace_moments: float32 [4, 16], replicated
Inputs may be any that keep to these rules, and one draw needn't show every extreme that they name: plan is a permutation of 0 to 31; stored block b is held by the device at gy index b // 4. The 4 lattice blocks of one device come from 4 different devices, and the 4 stored blocks of one device go to 4 different devices.
All inputs are finite; a program needn't handle non-finite values. No bound on the sum of `vacancy` on one device may be relied on, other than what follows from the above.
Results may differ from a plain program's by a relative error of at most 0.0003.
Values may be sent and summed in bfloat16 or wider, within the bound.
A program may use at most 64 MiB of HBM per device.

v0:
```python
import jax
import jax.numpy as jnp
from jax import lax
from jax.sharding import PartitionSpec as P

BLOCK = 128
R = 16
TERMS = 4
HOP_NEAR = 1.0
HOP_NEXT = 0.3
TWIST_COS = 0.4535961214255773
TWIST_SIN = 0.8912073600614354
SPREAD = 6.5
NEAR_A = ((0, 0), (-1, 0), (0, -1))
NEAR_B = ((0, 0), (1, 0), (0, 1))
SECOND = ((1, 0), (-1, 1), (0, -1))


def extended(block, sides, width):
    for axis, dim in sides:
        count = lax.axis_size(axis)
        forward = [(i, i + 1) for i in range(count - 1)]
        forward.append((count - 1, 0))
        backward = [(target, source) for source, target in forward]
        low = lax.ppermute(
            lax.slice_in_dim(block, block.shape[dim] - width, None, axis=dim), axis, forward
        )
        high = lax.ppermute(lax.slice_in_dim(block, 0, width, axis=dim), axis, backward)
        block = jnp.concatenate([low, block, high], axis=dim)
    return block


def collect_sum(fetch, field, shifts):
    total = fetch(field, shifts[0])
    for shift in shifts[1:]:
        total = total + fetch(field, shift)
    return total


def hamilton(fetch, real, imag, onsite, keep):
    backs = tuple(((-a, -b) for a, b in SECOND))
    out_real = []
    out_imag = []
    for sublat, chiral, bonds in ((0, 1.0, NEAR_A), (1, -1.0, NEAR_B)):
        other = 1 - sublat
        near_real = collect_sum(fetch, real[other], bonds)
        forward_real = collect_sum(fetch, real[sublat], SECOND)
        backward_real = collect_sum(fetch, real[sublat], backs)
        centre_real = fetch(real[sublat], (0, 0))
        mixed_real = TWIST_COS * (forward_real + backward_real)
        mixed_imag = chiral * TWIST_SIN * (forward_real - backward_real)
        level = onsite[sublat][None]
        if imag is None:
            result_imag = HOP_NEXT * mixed_imag
        else:
            near_imag = collect_sum(fetch, imag[other], bonds)
            forward_imag = collect_sum(fetch, imag[sublat], SECOND)
            backward_imag = collect_sum(fetch, imag[sublat], backs)
            centre_imag = fetch(imag[sublat], (0, 0))
            mixed_real = mixed_real - chiral * TWIST_SIN * (forward_imag - backward_imag)
            mixed_imag = mixed_imag + TWIST_COS * (forward_imag + backward_imag)
            result_imag = level * centre_imag - HOP_NEAR * near_imag + HOP_NEXT * mixed_imag
        result_real = level * centre_real - HOP_NEAR * near_real + HOP_NEXT * mixed_real
        factor = keep[sublat][None] / SPREAD
        out_real.append(result_real * factor)
        out_imag.append(result_imag * factor)
    return (jnp.stack(out_real), jnp.stack(out_imag))


def local(stored_vectors, disorder, vacancy, plan):
    column = lax.axis_index("gy")
    columns = lax.axis_size("gy")
    vectors = stored_vectors.shape[1]
    width_x = stored_vectors.shape[2]
    width_y = stored_vectors.shape[3]
    blocks_here = width_y // BLOCK
    total_blocks = plan.shape[0]
    wanted = lax.dynamic_slice_in_dim(plan, column * blocks_here, blocks_here)
    pieces = stored_vectors.reshape(2, vectors, width_x, blocks_here, BLOCK)
    held = column * blocks_here + jnp.arange(blocks_here, dtype=jnp.int32)
    matches = (plan[None, :] == held[:, None]).astype(jnp.int32)
    target = jnp.sum(jnp.arange(total_blocks, dtype=jnp.int32)[None, :] * matches, axis=1)
    target_device = target // blocks_here
    sender = (jnp.arange(columns, dtype=jnp.int32)[:, None] == target_device[None, :]).astype(
        jnp.bfloat16
    )
    outgoing = jnp.einsum(
        "pb,srxbc->psrxc", sender, pieces, preferred_element_type=jnp.float32
    ).astype(jnp.bfloat16)
    incoming = lax.all_to_all(outgoing, "gy", split_axis=0, concat_axis=0, tiled=True)
    source_device = wanted // blocks_here
    picker = (jnp.arange(columns, dtype=jnp.int32)[None, :] == source_device[:, None]).astype(
        jnp.bfloat16
    )
    arranged = jnp.einsum("kp,psrxc->srxkc", picker, incoming, preferred_element_type=jnp.float32)
    lattice = arranged.reshape(2, vectors, width_x, width_y)
    keep = vacancy.astype(jnp.float32)
    start = lattice * keep[:, None]
    sites_total = 2 * width_x * lax.axis_size("gx") * width_y * columns

    def operate(real, imag):
        if imag is None:
            joined = real[None]
        else:
            joined = jnp.stack([real, imag])
        padded = extended(joined, (("gx", 3), ("gy", 4)), 1)

        def fetch(field, shift):
            return field[
                :, 1 + shift[0] : 1 + shift[0] + width_x, 1 + shift[1] : 1 + shift[1] + width_y
            ]

        padded_imag = None if imag is None else padded[1]
        return hamilton(fetch, padded[0], padded_imag, disorder, keep)

    locals_list = []
    partials = []

    def record(field_real):
        product = start * field_real
        locals_list.append(jnp.sum(product, axis=1) / R)
        partial_value = jnp.sum(product, axis=(0, 2, 3))
        partials.append(partial_value)

    previous_real, previous_imag = (start, None)
    current_real, current_imag = operate(start, None)
    record(current_real)
    for term in range(1, TERMS):
        image_real, image_imag = operate(current_real, current_imag)
        next_real = 2.0 * image_real - previous_real
        if previous_imag is None:
            next_imag = 2.0 * image_imag
        else:
            next_imag = 2.0 * image_imag - previous_imag
        previous_real, previous_imag = (current_real, current_imag)
        current_real, current_imag = (next_real, next_imag)
        record(current_real)
    summed = lax.psum(jnp.stack(partials), ("gx", "gy"))
    return (jnp.stack(locals_list), summed / sites_total)


def solution(mesh):
    placed = (P(None, None, "gx", "gy"), P(None, "gx", "gy"), P(None, "gx", "gy"), P())
    return jax.shard_map(
        local,
        mesh=mesh,
        in_specs=placed,
        out_specs=(P(None, None, "gx", "gy"), P()),
        check_vma=False,
    )
```

profile of v0, /device:TPU:0, one launch (start us, length us, event | category | flops | bytes accessed | tf_op | source)
XLA Modules:
  0.0 175.9 jit_solution(6712092812964053303)
XLA Ops:
  0.7 0.9 select_reduce_fusion
  2.0 0.9 copy.10
  2.9 5.2 %all-to-all-start = ((bf16[8,2,16,8,128]{4,3,2,1,0:T(8,128)(2,1)}), bf16[8,2,16,8,128]{4,3,2,1,0:T(8,128)(2,1)S(1)}, u32[]{:S(2)}, u32[]{:S(2)}) async-start(bf16[8,2,16,8,128]{4,3,2,1,0:T(8,128)(2,1)} %copy.10), calls=%async_computation | async-start | bytes 1048576 | tf_op jit(solution)/shard_map/all_to_all | solution.py:90
  8.8 9.0 %all-to-all-done = bf16[8,2,16,8,128]{4,3,2,1,0:T(8,128)(2,1)S(1)} async-done(((bf16[8,2,16,8,128]{4,3,2,1,0:T(8,128)(2,1)}), bf16[8,2,16,8,128]{4,3,2,1,0:T(8,128)(2,1)S(1)}, u32[]{:S(2)}, u32[]{:S(2)}) %all-to-all-start) | async-done | bytes 524320 | tf_op jit(solution)/shard_map/all_to_all | solution.py:90
  18.6 1.6 collective-permute-start
  20.3 2.2 %collective-permute-start.1 = (f32[1,2,16,1,512]{4,3,2,1,0:T(1,128)S(1)}, f32[1,2,16,1,512]{4,3,2,1,0:T(1,128)S(1)}, u32[]{:S(2)}, u32[]{:S(2)}) collective-permute-start(f32[1,2,16,1,512]{4,3,2,1,0:T(1,128)S(1)} %get-tuple-element.54), channel_id=1, source_target_pairs={{8,0},{16,8},{24,16},{0,24},{9,1},{17,9},{25,17},{1,25},{10,2},{18... | collective-permute-start | bytes 196616 | tf_op jit(solution)/shard_map/ppermute | solution.py:28
  22.5 2.3 %collective-permute-done = f32[1,2,16,1,512]{4,3,2,1,0:T(1,128)S(1)} collective-permute-done((f32[1,2,16,1,512]{4,3,2,1,0:T(1,128)S(1)}, f32[1,2,16,1,512]{4,3,2,1,0:T(1,128)S(1)}, u32[]{:S(2)}, u32[]{:S(2)}) %collective-permute-start) | collective-permute-done | bytes 65568 | tf_op jit(solution)/shard_map/ppermute | solution.py:25
  25.5 2.6 %collective-permute-start.3 = (f32[1,2,16,10,1]{4,3,2,1,0:T(8,128)S(1)}, f32[1,2,16,10,1]{4,3,2,1,0:T(8,128)S(1)}, u32[]{:S(2)}, u32[]{:S(2)}) collective-permute-start(f32[1,2,16,10,1]{4,3,2,1,0:T(8,128)S(1)} %get-tuple-element.48), channel_id=1, source_target_pairs={{1,0},{2,1},{3,2},{4,3},{5,4},{6,5},{7,6},{0,7},{9,8},{10,9},{11,1... | collective-permute-start | bytes 3848 | tf_op jit(solution)/shard_map/ppermute | solution.py:28
  28.1 6.8 %collective-permute-done.2 = f32[1,2,16,10,1]{4,3,2,1,0:T(8,128)S(1)} collective-permute-done((f32[1,2,16,10,1]{4,3,2,1,0:T(8,128)S(1)}, f32[1,2,16,10,1]{4,3,2,1,0:T(8,128)S(1)}, u32[]{:S(2)}, u32[]{:S(2)}) %collective-permute-start.2) | collective-permute-done | bytes 1312 | tf_op jit(solution)/shard_map/ppermute | solution.py:25
  35.0 0.9 pad_maximum_fusion.3
  38.0 3.2 %collective-permute-start.5 = (f32[2,2,16,1,512]{4,3,2,1,0:T(1,128)S(1)}, f32[2,2,16,1,512]{4,3,2,1,0:T(1,128)S(1)}, u32[]{:S(2)}, u32[]{:S(2)}) collective-permute-start(f32[2,2,16,1,512]{4,3,2,1,0:T(1,128)S(1)} %get-tuple-element.46), channel_id=1, source_target_pairs={{8,0},{16,8},{24,16},{0,24},{9,1},{17,9},{25,17},{1,25},{10,2},{18... | collective-permute-start | bytes 393224 | tf_op jit(solution)/shard_map/ppermute | solution.py:28
  41.2 4.0 %collective-permute-done.4 = f32[2,2,16,1,512]{4,3,2,1,0:T(1,128)S(1)} collective-permute-done((f32[2,2,16,1,512]{4,3,2,1,0:T(1,128)S(1)}, f32[2,2,16,1,512]{4,3,2,1,0:T(1,128)S(1)}, u32[]{:S(2)}, u32[]{:S(2)}) %collective-permute-start.4) | collective-permute-done | bytes 131104 | tf_op jit(solution)/shard_map/ppermute | solution.py:25
  45.8 2.6 %collective-permute-start.7 = (f32[2,2,16,10,1]{4,3,2,1,0:T(8,128)S(1)}, f32[2,2,16,10,1]{4,3,2,1,0:T(8,128)S(1)}, u32[]{:S(2)}, u32[]{:S(2)}) collective-permute-start(f32[2,2,16,10,1]{4,3,2,1,0:T(8,128)S(1)} %get-tuple-element.33), channel_id=1, source_target_pairs={{1,0},{2,1},{3,2},{4,3},{5,4},{6,5},{7,6},{0,7},{9,8},{10,9},{11,1... | collective-permute-start | bytes 7688 | tf_op jit(solution)/shard_map/ppermute | solution.py:28
  48.5 11.6 %collective-permute-done.6 = f32[2,2,16,10,1]{4,3,2,1,0:T(8,128)S(1)} collective-permute-done((f32[2,2,16,10,1]{4,3,2,1,0:T(8,128)S(1)}, f32[2,2,16,10,1]{4,3,2,1,0:T(8,128)S(1)}, u32[]{:S(2)}, u32[]{:S(2)}) %collective-permute-start.6) | collective-permute-done | bytes 2592 | tf_op jit(solution)/shard_map/ppermute | solution.py:25
  60.0 1.9 %pad_maximum_fusion = f32[2,2,16,10,514]{4,3,2,1,0:T(8,128)S(1)} fusion(f32[2,2,16,10,1]{4,3,2,1,0:T(8,128)S(1)} %collective-permute-done.7, f32[2,2,16,1,512]{4,3,2,1,0:T(1,128)S(1)} %collective-permute-done.5, f32[1,2,16,8,512]{4,3,2,1,0:T(8,128)S(1)} %maximum_bitcast_fusion.1, f32[1,2,16,8,512]{4,3,2,1,0:T(8,128)S(1)} %maximum_bitcast_fusion, ...), kind=kLoop, calls=%fused_computation | loop fusion | flops 1644800 | bytes 2631680 | tf_op jit(solution)/shard_map/concatenate | solution.py:29
  62.1 0.8 add_multiply_fusion.3
  63.0 0.9 add_multiply_fusion.2
  63.8 0.8 multiply_bitcast_fusion.3
  64.7 0.9 multiply_bitcast_fusion.2
  65.9 2.1 %collective-permute-start.8 = (f32[2,2,16,1,512]{4,3,2,1,0:T(1,128)S(1)}, f32[2,2,16,1,512]{4,3,2,1,0:T(1,128)S(1)}, u32[]{:S(2)}, u32[]{:S(2)}) collective-permute-start(f32[2,2,16,1,512]{4,3,2,1,0:T(1,128)S(1)} %get-tuple-element.43), channel_id=1, source_target_pairs={{0,8},{8,16},{16,24},{24,0},{1,9},{9,17},{17,25},{25,1},{2,10},{10... | collective-permute-start | bytes 393224 | tf_op jit(solution)/shard_map/ppermute | solution.py:25
  68.0 1.8 %collective-permute-start.9 = (f32[2,2,16,1,512]{4,3,2,1,0:T(1,128)S(1)}, f32[2,2,16,1,512]{4,3,2,1,0:T(1,128)S(1)}, u32[]{:S(2)}, u32[]{:S(2)}) collective-permute-start(f32[2,2,16,1,512]{4,3,2,1,0:T(1,128)S(1)} %get-tuple-element.44), channel_id=1, source_target_pairs={{8,0},{16,8},{24,16},{0,24},{9,1},{17,9},{25,17},{1,25},{10,2},{18... | collective-permute-start | bytes 393224 | tf_op jit(solution)/shard_map/ppermute | solution.py:28
  69.8 4.4 %collective-permute-done.8 = f32[2,2,16,1,512]{4,3,2,1,0:T(1,128)S(1)} collective-permute-done((f32[2,2,16,1,512]{4,3,2,1,0:T(1,128)S(1)}, f32[2,2,16,1,512]{4,3,2,1,0:T(1,128)S(1)}, u32[]{:S(2)}, u32[]{:S(2)}) %collective-permute-start.8) | collective-permute-done | bytes 131104 | tf_op jit(solution)/shard_map/ppermute | solution.py:25
  74.2 1.9 %collective-permute-done.9 = f32[2,2,16,1,512]{4,3,2,1,0:T(1,128)S(1)} collective-permute-done((f32[2,2,16,1,512]{4,3,2,1,0:T(1,128)S(1)}, f32[2,2,16,1,512]{4,3,2,1,0:T(1,128)S(1)}, u32[]{:S(2)}, u32[]{:S(2)}) %collective-permute-start.9) | collective-permute-done | bytes 131104 | tf_op jit(solution)/shard_map/ppermute | solution.py:28
  76.5 2.6 %collective-permute-start.11 = (f32[2,2,16,10,1]{4,3,2,1,0:T(8,128)S(1)}, f32[2,2,16,10,1]{4,3,2,1,0:T(8,128)S(1)}, u32[]{:S(2)}, u32[]{:S(2)}) collective-permute-start(f32[2,2,16,10,1]{4,3,2,1,0:T(8,128)S(1)} %get-tuple-element.31), channel_id=1, source_target_pairs={{1,0},{2,1},{3,2},{4,3},{5,4},{6,5},{7,6},{0,7},{9,8},{10,9},{11,1... | collective-permute-start | bytes 7688 | tf_op jit(solution)/shard_map/ppermute | solution.py:28
  79.2 12.5 %collective-permute-done.10 = f32[2,2,16,10,1]{4,3,2,1,0:T(8,128)S(1)} collective-permute-done((f32[2,2,16,10,1]{4,3,2,1,0:T(8,128)S(1)}, f32[2,2,16,10,1]{4,3,2,1,0:T(8,128)S(1)}, u32[]{:S(2)}, u32[]{:S(2)}) %collective-permute-start.10) | collective-permute-done | bytes 2592 | tf_op jit(solution)/shard_map/ppermute | solution.py:25
  91.6 1.9 %pad_maximum_fusion.1 = f32[2,2,16,10,514]{4,3,2,1,0:T(8,128)S(1)} fusion(f32[2,2,16,10,1]{4,3,2,1,0:T(8,128)S(1)} %collective-permute-done.11, f32[2,2,16,1,512]{4,3,2,1,0:T(1,128)S(1)} %collective-permute-done.9, f32[1,2,16,8,512]{4,3,2,1,0:T(8,128)S(1)} %maximum_multiply_fusion.2, f32[1,2,16,8,512]{4,3,2,1,0:T(8,128)S(1)} %fusion.1, ...), kind=kLoop, calls=%fused_computation.1 | loop fusion | flops 1644800 | bytes 2631680 | tf_op jit(solution)/shard_map/concatenate | solution.py:29
  93.7 0.8 add_multiply_fusion.1
  94.6 0.9 add_multiply_fusion
  95.5 0.8 multiply_bitcast_fusion.1
  96.3 0.9 multiply_bitcast_fusion
  97.4 0.9 pad_maximum_fusion.20
  98.9 3.2 %collective-permute-start.13 = (f32[2,2,16,1,512]{4,3,2,1,0:T(1,128)}, f32[2,2,16,1,512]{4,3,2,1,0:T(1,128)}, u32[]{:S(2)}, u32[]{:S(2)}) collective-permute-start(f32[2,2,16,1,512]{4,3,2,1,0:T(1,128)} %get-tuple-element.42), channel_id=1, source_target_pairs={{8,0},{16,8},{24,16},{0,24},{9,1},{17,9},{25,17},{1,25},{10,2},{18... | collective-permute-start | bytes 393224 | tf_op jit(solution)/shard_map/ppermute | solution.py:28
  102.7 0.8 stack.134
  104.2 1.0 constant_dynamic-update-slice_fusion.1
  105.3 1.5 collective-permute-done.12
  107.0 2.1 %pad_maximum_fusion.7 = (f32[2,2,16,10,1]{4,3,2,1,0:T(8,128)}, f32[2,2,16,10,1]{4,3,2,1,0:T(8,128)}) fusion(f32[2,2,16,1,512]{4,3,2,1,0:T(1,128)} %collective-permute-done.13, f32[2,2,16,1,512]{4,3,2,1,0:T(1,128)} %collective-permute-done.12, f32[1,2,16,8,512]{4,3,2,1,0:T(8,128)S(1)} %fusion.5, f32[1,2,16,8,512]{4,3,2,1,0:T(8,128)S(1)} %fusion.4), kind=kLoop, calls=%fused_computation.23 | loop fusion | flops 3840 | bytes 1315840 | tf_op jit(solution)/shard_map/slice | solution.py:26
  109.1 2.6 %collective-permute-start.15 = (f32[2,2,16,10,1]{4,3,2,1,0:T(8,128)}, f32[2,2,16,10,1]{4,3,2,1,0:T(8,128)}, u32[]{:S(2)}, u32[]{:S(2)}) collective-permute-start(f32[2,2,16,10,1]{4,3,2,1,0:T(8,128)} %get-tuple-element.29), channel_id=1, source_target_pairs={{1,0},{2,1},{3,2},{4,3},{5,4},{6,5},{7,6},{0,7},{9,8},{10,9},{11,1... | collective-permute-start | bytes 7688 | tf_op jit(solution)/shard_map/ppermute | solution.py:28
  111.8 0.9 stack.146
  112.7 0.8 stack.147
  114.3 0.8 stack.157
  115.1 9.4 %collective-permute-done.14 = f32[2,2,16,10,1]{4,3,2,1,0:T(8,128)} collective-permute-done((f32[2,2,16,10,1]{4,3,2,1,0:T(8,128)}, f32[2,2,16,10,1]{4,3,2,1,0:T(8,128)}, u32[]{:S(2)}, u32[]{:S(2)}) %collective-permute-start.14) | collective-permute-done | bytes 2592 | tf_op jit(solution)/shard_map/ppermute | solution.py:25
  124.5 3.1 %pad_maximum_fusion.2 = f32[2,2,16,10,514]{4,3,2,1,0:T(8,128)S(1)} fusion(f32[2,2,16,10,1]{4,3,2,1,0:T(8,128)} %collective-permute-done.15, f32[2,2,16,1,512]{4,3,2,1,0:T(1,128)} %collective-permute-done.13, f32[1,2,16,8,512]{4,3,2,1,0:T(8,128)S(1)} %fusion.5, f32[1,2,16,8,512]{4,3,2,1,0:T(8,128)S(1)} %fusion.4, ...), kind=kLoop, calls=%fused_computation.2 | loop fusion | flops 1644800 | bytes 2631680 | tf_op jit(solution)/shard_map/concatenate | solution.py:29
  127.9 0.8 fusion.23
  128.7 0.8 stack.172
  129.5 2.4 %fusion.14 = f32[16,8,512]{2,1,0:T(8,128)} fusion(f32[16,10,514]{2,1,0:T(8,128)S(1)} %get-tuple-element.17, f32[16,10,514]{2,1,0:T(8,128)S(1)} %get-tuple-element.18, f32[16,10,514]{2,1,0:T(8,128)S(1)} %get-tuple-element.19, f32[8,512]{1,0:T(8,128)S(1)} %get-tuple-element.60, f32[8,512]{1,0:T(8,128)} %copy-done.5), kind=kLoop, calls=%fused_computation.58 | loop fusion | flops 1310720 | bytes 4489216 | tf_op jit(solution)/shard_map/mul | solution.py:65
  131.9 1.0 stack.173
  132.9 2.0 %fusion.38 = (f32[16]{0:T(128)S(1)}, f32[2,8,4,128]{3,2,1,0:T(4,128)S(1)}, f32[2,16,8,4,128]{4,3,2,1,0:T(4,128)S(1)}, f32[2,16,8,4,128]{4,3,2,1,0:T(4,128)S(1)}, f32[2,16,8,4,128]{4,3,2,1,0:T(4,128)S(1)}) fusion(f32[2,16,8,4,128]{4,3,2,1,0:T(4,128)S(1)} %copy-done.2, f32[2,16,8,4,128]{4,3,2,1,0:T(4,128)S(1)} %convolution_bitcast_fusion, ...), kind=kLoop, calls=%fused_computation.148 | loop fusion | flops 2088944 | bytes 4259904 | tf_op jit(solution)/shard_map/reduce_sum | solution.py:122
  135.7 38.9 %psum.7 = f32[4,16]{1,0:T(4,128)S(1)} all-reduce(f32[4,16]{1,0:T(4,128)S(1)} %pad_maximum_fusion.26), channel_id=1, replica_groups=mesh['gx'=4,'gy'=8] {'gx','gy'}, use_global_device_ids=true, to_apply=%region_9.10 | all-reduce | flops 64 | bytes 512 | tf_op jit(solution)/shard_map/psum | solution.py:138
  (79 shorter events, 12.0 us)
Async XLA Ops:
  0.6 1.0 copy-start
  0.6 7.5 %copy-start.9 = (s32[32]{0:T(128)S(1)}, s32[32]{0:T(128)}, u32[]{:S(2)}) copy-start(s32[32]{0:T(128)} %param.7) | copy-start | bytes 388
  0.7 7.6 %copy-start.7 = (s32[2,8,512]{2,1,0:T(8,128)S(1)}, s32[2,8,512]{2,1,0:T(8,128)}, u32[]{:S(2)}) copy-start(s32[2,8,512]{2,1,0:T(8,128)} %param.6) | copy-start | bytes 98308
  2.0 20.5 %copy-start.8 = (f32[2,8,512]{2,1,0:T(8,128)S(1)}, f32[2,8,512]{2,1,0:T(8,128)}, u32[]{:S(2)}) copy-start(f32[2,8,512]{2,1,0:T(8,128)} %param.5) | copy-start | bytes 98308
  2.9 14.9 %all-to-all-start = ((bf16[8,2,16,8,128]{4,3,2,1,0:T(8,128)(2,1)}), bf16[8,2,16,8,128]{4,3,2,1,0:T(8,128)(2,1)S(1)}, u32[]{:S(2)}, u32[]{:S(2)}) async-start(bf16[8,2,16,8,128]{4,3,2,1,0:T(8,128)(2,1)} %copy.10), calls=%async_computation | async-start | bytes 1048576 | tf_op jit(solution)/shard_map/all_to_all | solution.py:90
  18.6 6.2 %collective-permute-start = (f32[1,2,16,1,512]{4,3,2,1,0:T(1,128)S(1)}, f32[1,2,16,1,512]{4,3,2,1,0:T(1,128)S(1)}, u32[]{:S(2)}, u32[]{:S(2)}) collective-permute-start(f32[1,2,16,1,512]{4,3,2,1,0:T(1,128)S(1)} %get-tuple-element.53), channel_id=1, source_target_pairs={{0,8},{8,16},{16,24},{24,0},{1,9},{9,17},{17,25},{25,1},{2,10},{10... | collective-permute-start | bytes 196616 | tf_op jit(solution)/shard_map/ppermute | solution.py:25
  20.3 5.0 %collective-permute-start.1 = (f32[1,2,16,1,512]{4,3,2,1,0:T(1,128)S(1)}, f32[1,2,16,1,512]{4,3,2,1,0:T(1,128)S(1)}, u32[]{:S(2)}, u32[]{:S(2)}) collective-permute-start(f32[1,2,16,1,512]{4,3,2,1,0:T(1,128)S(1)} %get-tuple-element.54), channel_id=1, source_target_pairs={{8,0},{16,8},{24,16},{0,24},{9,1},{17,9},{25,17},{1,25},{10,2},{18... | collective-permute-start | bytes 196616 | tf_op jit(solution)/shard_map/ppermute | solution.py:28
  22.5 73.8 %copy-start.5 = (f32[8,512]{1,0:T(8,128)}, f32[8,512]{1,0:T(8,128)S(1)}, u32[]{:S(2)}) copy-start(f32[8,512]{1,0:T(8,128)S(1)} %get-tuple-element.66) | copy-start | bytes 49156
  25.4 9.6 %collective-permute-start.2 = (f32[1,2,16,10,1]{4,3,2,1,0:T(8,128)S(1)}, f32[1,2,16,10,1]{4,3,2,1,0:T(8,128)S(1)}, u32[]{:S(2)}, u32[]{:S(2)}) collective-permute-start(f32[1,2,16,10,1]{4,3,2,1,0:T(8,128)S(1)} %get-tuple-element.47), channel_id=1, source_target_pairs={{0,1},{1,2},{2,3},{3,4},{4,5},{5,6},{6,7},{7,0},{8,9},{9,10},{10,1... | collective-permute-start | bytes 3848 | tf_op jit(solution)/shard_map/ppermute | solution.py:25
  25.5 9.5 %collective-permute-start.3 = (f32[1,2,16,10,1]{4,3,2,1,0:T(8,128)S(1)}, f32[1,2,16,10,1]{4,3,2,1,0:T(8,128)S(1)}, u32[]{:S(2)}, u32[]{:S(2)}) collective-permute-start(f32[1,2,16,10,1]{4,3,2,1,0:T(8,128)S(1)} %get-tuple-element.48), channel_id=1, source_target_pairs={{1,0},{2,1},{3,2},{4,3},{5,4},{6,5},{7,6},{0,7},{9,8},{10,9},{11,1... | collective-permute-start | bytes 3848 | tf_op jit(solution)/shard_map/ppermute | solution.py:28
  37.3 7.9 %collective-permute-start.4 = (f32[2,2,16,1,512]{4,3,2,1,0:T(1,128)S(1)}, f32[2,2,16,1,512]{4,3,2,1,0:T(1,128)S(1)}, u32[]{:S(2)}, u32[]{:S(2)}) collective-permute-start(f32[2,2,16,1,512]{4,3,2,1,0:T(1,128)S(1)} %get-tuple-element.45), channel_id=1, source_target_pairs={{0,8},{8,16},{16,24},{24,0},{1,9},{9,17},{17,25},{25,1},{2,10},{10... | collective-permute-start | bytes 393224 | tf_op jit(solution)/shard_map/ppermute | solution.py:25
  38.0 7.4 %collective-permute-start.5 = (f32[2,2,16,1,512]{4,3,2,1,0:T(1,128)S(1)}, f32[2,2,16,1,512]{4,3,2,1,0:T(1,128)S(1)}, u32[]{:S(2)}, u32[]{:S(2)}) collective-permute-start(f32[2,2,16,1,512]{4,3,2,1,0:T(1,128)S(1)} %get-tuple-element.46), channel_id=1, source_target_pairs={{8,0},{16,8},{24,16},{0,24},{9,1},{17,9},{25,17},{1,25},{10,2},{18... | collective-permute-start | bytes 393224 | tf_op jit(solution)/shard_map/ppermute | solution.py:28
  45.8 14.2 %collective-permute-start.6 = (f32[2,2,16,10,1]{4,3,2,1,0:T(8,128)S(1)}, f32[2,2,16,10,1]{4,3,2,1,0:T(8,128)S(1)}, u32[]{:S(2)}, u32[]{:S(2)}) collective-permute-start(f32[2,2,16,10,1]{4,3,2,1,0:T(8,128)S(1)} %get-tuple-element.32), channel_id=1, source_target_pairs={{0,1},{1,2},{2,3},{3,4},{4,5},{5,6},{6,7},{7,0},{8,9},{9,10},{10,1... | collective-permute-start | bytes 7688 | tf_op jit(solution)/shard_map/ppermute | solution.py:25
  45.8 14.2 %collective-permute-start.7 = (f32[2,2,16,10,1]{4,3,2,1,0:T(8,128)S(1)}, f32[2,2,16,10,1]{4,3,2,1,0:T(8,128)S(1)}, u32[]{:S(2)}, u32[]{:S(2)}) collective-permute-start(f32[2,2,16,10,1]{4,3,2,1,0:T(8,128)S(1)} %get-tuple-element.33), channel_id=1, source_target_pairs={{1,0},{2,1},{3,2},{4,3},{5,4},{6,5},{7,6},{0,7},{9,8},{10,9},{11,1... | collective-permute-start | bytes 7688 | tf_op jit(solution)/shard_map/ppermute | solution.py:28
  65.9 8.3 %collective-permute-start.8 = (f32[2,2,16,1,512]{4,3,2,1,0:T(1,128)S(1)}, f32[2,2,16,1,512]{4,3,2,1,0:T(1,128)S(1)}, u32[]{:S(2)}, u32[]{:S(2)}) collective-permute-start(f32[2,2,16,1,512]{4,3,2,1,0:T(1,128)S(1)} %get-tuple-element.43), channel_id=1, source_target_pairs={{0,8},{8,16},{16,24},{24,0},{1,9},{9,17},{17,25},{25,1},{2,10},{10... | collective-permute-start | bytes 393224 | tf_op jit(solution)/shard_map/ppermute | solution.py:25
  68.0 8.1 %collective-permute-start.9 = (f32[2,2,16,1,512]{4,3,2,1,0:T(1,128)S(1)}, f32[2,2,16,1,512]{4,3,2,1,0:T(1,128)S(1)}, u32[]{:S(2)}, u32[]{:S(2)}) collective-permute-start(f32[2,2,16,1,512]{4,3,2,1,0:T(1,128)S(1)} %get-tuple-element.44), channel_id=1, source_target_pairs={{8,0},{16,8},{24,16},{0,24},{9,1},{17,9},{25,17},{1,25},{10,2},{18... | collective-permute-start | bytes 393224 | tf_op jit(solution)/shard_map/ppermute | solution.py:28
  76.5 15.2 %collective-permute-start.10 = (f32[2,2,16,10,1]{4,3,2,1,0:T(8,128)S(1)}, f32[2,2,16,10,1]{4,3,2,1,0:T(8,128)S(1)}, u32[]{:S(2)}, u32[]{:S(2)}) collective-permute-start(f32[2,2,16,10,1]{4,3,2,1,0:T(8,128)S(1)} %get-tuple-element.30), channel_id=1, source_target_pairs={{0,1},{1,2},{2,3},{3,4},{4,5},{5,6},{6,7},{7,0},{8,9},{9,10},{10,1... | collective-permute-start | bytes 7688 | tf_op jit(solution)/shard_map/ppermute | solution.py:25
  76.5 15.1 %collective-permute-start.11 = (f32[2,2,16,10,1]{4,3,2,1,0:T(8,128)S(1)}, f32[2,2,16,10,1]{4,3,2,1,0:T(8,128)S(1)}, u32[]{:S(2)}, u32[]{:S(2)}) collective-permute-start(f32[2,2,16,10,1]{4,3,2,1,0:T(8,128)S(1)} %get-tuple-element.31), channel_id=1, source_target_pairs={{1,0},{2,1},{3,2},{4,3},{5,4},{6,5},{7,6},{0,7},{9,8},{10,9},{11,1... | collective-permute-start | bytes 7688 | tf_op jit(solution)/shard_map/ppermute | solution.py:28
  97.2 4.9 %copy-start.6 = (f32[2,8,4,128]{3,1,2,0:T(8,128)S(1)}, f32[2,8,4,128]{3,1,2,0:T(8,128)}, u32[]{:S(2)}) copy-start(f32[2,8,4,128]{3,1,2,0:T(8,128)} %get-tuple-element.55) | copy-start | bytes 98308
  98.3 8.5 %collective-permute-start.12 = (f32[2,2,16,1,512]{4,3,2,1,0:T(1,128)}, f32[2,2,16,1,512]{4,3,2,1,0:T(1,128)}, u32[]{:S(2)}, u32[]{:S(2)}) collective-permute-start(f32[2,2,16,1,512]{4,3,2,1,0:T(1,128)} %get-tuple-element.41), channel_id=1, source_target_pairs={{0,8},{8,16},{16,24},{24,0},{1,9},{9,17},{17,25},{25,1},{2,10},{10... | collective-permute-start | bytes 393224 | tf_op jit(solution)/shard_map/ppermute | solution.py:25
  98.9 8.1 %collective-permute-start.13 = (f32[2,2,16,1,512]{4,3,2,1,0:T(1,128)}, f32[2,2,16,1,512]{4,3,2,1,0:T(1,128)}, u32[]{:S(2)}, u32[]{:S(2)}) collective-permute-start(f32[2,2,16,1,512]{4,3,2,1,0:T(1,128)} %get-tuple-element.42), channel_id=1, source_target_pairs={{8,0},{16,8},{24,16},{0,24},{9,1},{17,9},{25,17},{1,25},{10,2},{18... | collective-permute-start | bytes 393224 | tf_op jit(solution)/shard_map/ppermute | solution.py:28
  104.2 7.5 %copy-start.4 = (f32[1,16,8,4,128]{4,3,2,1,0:T(4,128)S(1)}, f32[1,16,8,4,128]{4,3,2,1,0:T(4,128)}, u32[]{:S(2)}) copy-start(f32[1,16,8,4,128]{4,3,2,1,0:T(4,128)} %stack.135) | copy-start | bytes 786436
  109.1 15.4 %collective-permute-start.14 = (f32[2,2,16,10,1]{4,3,2,1,0:T(8,128)}, f32[2,2,16,10,1]{4,3,2,1,0:T(8,128)}, u32[]{:S(2)}, u32[]{:S(2)}) collective-permute-start(f32[2,2,16,10,1]{4,3,2,1,0:T(8,128)} %get-tuple-element.28), channel_id=1, source_target_pairs={{0,1},{1,2},{2,3},{3,4},{4,5},{5,6},{6,7},{7,0},{8,9},{9,10},{10,1... | collective-permute-start | bytes 7688 | tf_op jit(solution)/shard_map/ppermute | solution.py:25
  109.1 15.4 %collective-permute-start.15 = (f32[2,2,16,10,1]{4,3,2,1,0:T(8,128)}, f32[2,2,16,10,1]{4,3,2,1,0:T(8,128)}, u32[]{:S(2)}, u32[]{:S(2)}) collective-permute-start(f32[2,2,16,10,1]{4,3,2,1,0:T(8,128)} %get-tuple-element.29), channel_id=1, source_target_pairs={{1,0},{2,1},{3,2},{4,3},{5,4},{6,5},{7,6},{0,7},{9,8},{10,9},{11,1... | collective-permute-start | bytes 7688 | tf_op jit(solution)/shard_map/ppermute | solution.py:28
  111.8 12.7 %copy-start.1 = (f32[2,16,8,4,128]{4,3,2,1,0:T(4,128)}, f32[2,16,8,4,128]{4,3,2,1,0:T(4,128)S(1)}, u32[]{:S(2)}) copy-start(f32[2,16,8,4,128]{4,3,2,1,0:T(4,128)S(1)} %constant_dynamic-update-slice_fusion) | copy-start | bytes 1572868
  129.5 3.4 %copy-start.2 = (f32[2,16,8,4,128]{4,3,2,1,0:T(4,128)S(1)}, f32[2,16,8,4,128]{4,3,2,1,0:T(4,128)}, u32[]{:S(2)}) copy-start(f32[2,16,8,4,128]{4,3,2,1,0:T(4,128)} %copy-done.1) | copy-start | bytes 1572868
  129.5 3.4 %copy-start.3 = (f32[1,16,8,4,128]{4,3,2,1,0:T(4,128)S(1)}, f32[1,16,8,4,128]{4,3,2,1,0:T(4,128)}, u32[]{:S(2)}) copy-start(f32[1,16,8,4,128]{4,3,2,1,0:T(4,128)} %stack.146) | copy-start | bytes 786436
where the time goes:
time: 176 us
  waiting for transfers between devices  64.3 us (37%)
  blocking collectives  38.9 us (22%)
  starting transfers between devices  31.4 us (18%)
  other arithmetic  29.2 us (17%)
  local copies, waits for them, and re-layouts  10.3 us (6%)
    ppermute x8, waiting for transfers between devices, extended(): lax.ppermute(lax.slice_in_dim(block, block.shape[dim] - width, None, axis...  52.5 us
    psum x1, blocking collectives, local(): summed = lax.psum(jnp.stack(partials), ('gx', 'gy'))  38.9 us
    ppermute x8, starting transfers between devices, extended(): lax.ppermute(lax.slice_in_dim(block, 0, width, axis=dim), axis, backward)  21 us
    all_to_all x1, waiting for transfers between devices, local(): lax.all_to_all(outgoing, 'gy', split_axis=0, concat_axis=0, tiled=True)  8.99 us
    concatenate x4, other arithmetic, extended(): block = jnp.concatenate([low, block, high], axis=dim)  7.79 us
    mul x8, other arithmetic, hamilton(): out_real.append(result_real * factor)  7.05 us
    another operation x9, local copies, waits for them, and re-layouts, hamilton(): return (jnp.stack(out_real), jnp.stack(out_imag))  6.65 us
    all_to_all x1, starting transfers between devices, local(): lax.all_to_all(outgoing, 'gy', split_axis=0, concat_axis=0, tiled=True)  5.2 us
  transfers between devices with their start and end apart: 17, of which 13 were waited for; matrix products, arithmetic and copies ran while one was open for 4% of the time, Pallas kernels for 0%

commit v1 on v0

--- a/solution.py
+++ b/solution.py
@@ -135,7 +135,7 @@
         previous_real, previous_imag = (current_real, current_imag)
         current_real, current_imag = (next_real, next_imag)
         record(current_real)
-    summed = lax.psum(jnp.stack(partials), ("gx", "gy"))
+    summed = lax.psum(lax.psum(jnp.stack(partials), "gx"), "gy")
     return (jnp.stack(locals_list), summed / sites_total)
 
 

time: 176 us -> 160 us (0.909)
  blocking collectives: 38.9 us -> 22.3 us
    psum x1 -> x2, blocking collectives: 38.9 us -> 22.3 us  [local(): summed = lax.psum(lax.psum(jnp.stack(partials), 'gx'), 'gy')]
  transfers between devices with their start and end apart: 17 -> 17, of which waited for: 13 -> 13; matrix products, arithmetic and copies ran while one was open for 4% -> 5% of each run, Pallas kernels for 0% -> 0%
where the time goes in v1:
time: 160 us; the launch traced here: 159 us
  waiting for transfers between devices  64.2 us (40%)
  starting transfers between devices  31.4 us (20%)
  other arithmetic  29.2 us (18%)
  blocking collectives  22.3 us (14%)
  local copies, waits for them, and re-layouts  10.4 us (6%)
    ppermute x8, waiting for transfers between devices, extended(): lax.ppermute(lax.slice_in_dim(block, block.shape[dim] - width, None, axis...  52.4 us
    psum x2, blocking collectives, local(): summed = lax.psum(lax.psum(jnp.stack(partials), 'gx'), 'gy')  22.3 us
    ppermute x8, starting transfers between devices, extended(): lax.ppermute(lax.slice_in_dim(block, 0, width, axis=dim), axis, backward)  21 us
    all_to_all x1, waiting for transfers between devices, local(): lax.all_to_all(outgoing, 'gy', split_axis=0, concat_axis=0, tiled=True)  9 us
    concatenate x4, other arithmetic, extended(): block = jnp.concatenate([low, block, high], axis=dim)  7.79 us
    mul x8, other arithmetic, hamilton(): out_real.append(result_real * factor)  7.05 us
    another operation x9, local copies, waits for them, and re-layouts, hamilton(): return (jnp.stack(out_real), jnp.stack(out_imag))  6.7 us
    all_to_all x1, starting transfers between devices, local(): lax.all_to_all(outgoing, 'gy', split_axis=0, concat_axis=0, tiled=True)  5.2 us
  transfers between devices with their start and end apart: 17, of which 13 were waited for; matrix products, arithmetic and copies ran while one was open for 5% of the time, Pallas kernels for 0%

profile of v1, /device:TPU:0, one launch (start us, length us, event | category | flops | bytes accessed | tf_op | source)
XLA Modules:
  0.0 159.4 jit_solution(12380930422159634014)
XLA Ops:
  0.7 0.9 select_reduce_fusion
  2.0 0.9 copy.10
  2.9 5.2 %all-to-all-start = ((bf16[8,2,16,8,128]{4,3,2,1,0:T(8,128)(2,1)}), bf16[8,2,16,8,128]{4,3,2,1,0:T(8,128)(2,1)S(1)}, u32[]{:S(2)}, u32[]{:S(2)}) async-start(bf16[8,2,16,8,128]{4,3,2,1,0:T(8,128)(2,1)} %copy.10), calls=%async_computation | async-start | bytes 1048576 | tf_op jit(solution)/shard_map/all_to_all | solution.py:90
  8.8 9.0 %all-to-all-done = bf16[8,2,16,8,128]{4,3,2,1,0:T(8,128)(2,1)S(1)} async-done(((bf16[8,2,16,8,128]{4,3,2,1,0:T(8,128)(2,1)}), bf16[8,2,16,8,128]{4,3,2,1,0:T(8,128)(2,1)S(1)}, u32[]{:S(2)}, u32[]{:S(2)}) %all-to-all-start) | async-done | bytes 524320 | tf_op jit(solution)/shard_map/all_to_all | solution.py:90
  18.6 1.6 %collective-permute-start = (f32[1,2,16,1,512]{4,3,2,1,0:T(1,128)S(1)}, f32[1,2,16,1,512]{4,3,2,1,0:T(1,128)S(1)}, u32[]{:S(2)}, u32[]{:S(2)}) collective-permute-start(f32[1,2,16,1,512]{4,3,2,1,0:T(1,128)S(1)} %get-tuple-element.53), channel_id=1, source_target_pairs={{0,8},{8,16},{16,24},{24,0},{1,9},{9,17},{17,25},{25,1},{2,10},{10... | collective-permute-start | bytes 196616 | tf_op jit(solution)/shard_map/ppermute | solution.py:25
  20.3 2.2 %collective-permute-start.1 = (f32[1,2,16,1,512]{4,3,2,1,0:T(1,128)S(1)}, f32[1,2,16,1,512]{4,3,2,1,0:T(1,128)S(1)}, u32[]{:S(2)}, u32[]{:S(2)}) collective-permute-start(f32[1,2,16,1,512]{4,3,2,1,0:T(1,128)S(1)} %get-tuple-element.54), channel_id=1, source_target_pairs={{8,0},{16,8},{24,16},{0,24},{9,1},{17,9},{25,17},{1,25},{10,2},{18... | collective-permute-start | bytes 196616 | tf_op jit(solution)/shard_map/ppermute | solution.py:28
  22.5 2.3 %collective-permute-done = f32[1,2,16,1,512]{4,3,2,1,0:T(1,128)S(1)} collective-permute-done((f32[1,2,16,1,512]{4,3,2,1,0:T(1,128)S(1)}, f32[1,2,16,1,512]{4,3,2,1,0:T(1,128)S(1)}, u32[]{:S(2)}, u32[]{:S(2)}) %collective-permute-start) | collective-permute-done | bytes 65568 | tf_op jit(solution)/shard_map/ppermute | solution.py:25
  25.5 2.6 %collective-permute-start.3 = (f32[1,2,16,10,1]{4,3,2,1,0:T(8,128)S(1)}, f32[1,2,16,10,1]{4,3,2,1,0:T(8,128)S(1)}, u32[]{:S(2)}, u32[]{:S(2)}) collective-permute-start(f32[1,2,16,10,1]{4,3,2,1,0:T(8,128)S(1)} %get-tuple-element.48), channel_id=1, source_target_pairs={{1,0},{2,1},{3,2},{4,3},{5,4},{6,5},{7,6},{0,7},{9,8},{10,9},{11,1... | collective-permute-start | bytes 3848 | tf_op jit(solution)/shard_map/ppermute | solution.py:28
  28.1 6.8 %collective-permute-done.2 = f32[1,2,16,10,1]{4,3,2,1,0:T(8,128)S(1)} collective-permute-done((f32[1,2,16,10,1]{4,3,2,1,0:T(8,128)S(1)}, f32[1,2,16,10,1]{4,3,2,1,0:T(8,128)S(1)}, u32[]{:S(2)}, u32[]{:S(2)}) %collective-permute-start.2) | collective-permute-done | bytes 1312 | tf_op jit(solution)/shard_map/ppermute | solution.py:25
  35.0 0.9 pad_maximum_fusion.3
  38.0 3.2 %collective-permute-start.5 = (f32[2,2,16,1,512]{4,3,2,1,0:T(1,128)S(1)}, f32[2,2,16,1,512]{4,3,2,1,0:T(1,128)S(1)}, u32[]{:S(2)}, u32[]{:S(2)}) collective-permute-start(f32[2,2,16,1,512]{4,3,2,1,0:T(1,128)S(1)} %get-tuple-element.46), channel_id=1, source_target_pairs={{8,0},{16,8},{24,16},{0,24},{9,1},{17,9},{25,17},{1,25},{10,2},{18... | collective-permute-start | bytes 393224 | tf_op jit(solution)/shard_map/ppermute | solution.py:28
  41.2 4.0 %collective-permute-done.4 = f32[2,2,16,1,512]{4,3,2,1,0:T(1,128)S(1)} collective-permute-done((f32[2,2,16,1,512]{4,3,2,1,0:T(1,128)S(1)}, f32[2,2,16,1,512]{4,3,2,1,0:T(1,128)S(1)}, u32[]{:S(2)}, u32[]{:S(2)}) %collective-permute-start.4) | collective-permute-done | bytes 131104 | tf_op jit(solution)/shard_map/ppermute | solution.py:25
  45.8 2.6 %collective-permute-start.7 = (f32[2,2,16,10,1]{4,3,2,1,0:T(8,128)S(1)}, f32[2,2,16,10,1]{4,3,2,1,0:T(8,128)S(1)}, u32[]{:S(2)}, u32[]{:S(2)}) collective-permute-start(f32[2,2,16,10,1]{4,3,2,1,0:T(8,128)S(1)} %get-tuple-element.33), channel_id=1, source_target_pairs={{1,0},{2,1},{3,2},{4,3},{5,4},{6,5},{7,6},{0,7},{9,8},{10,9},{11,1... | collective-permute-start | bytes 7688 | tf_op jit(solution)/shard_map/ppermute | solution.py:28
  48.5 11.6 %collective-permute-done.6 = f32[2,2,16,10,1]{4,3,2,1,0:T(8,128)S(1)} collective-permute-done((f32[2,2,16,10,1]{4,3,2,1,0:T(8,128)S(1)}, f32[2,2,16,10,1]{4,3,2,1,0:T(8,128)S(1)}, u32[]{:S(2)}, u32[]{:S(2)}) %collective-permute-start.6) | collective-permute-done | bytes 2592 | tf_op jit(solution)/shard_map/ppermute | solution.py:25
  60.0 1.9 %pad_maximum_fusion = f32[2,2,16,10,514]{4,3,2,1,0:T(8,128)S(1)} fusion(f32[2,2,16,10,1]{4,3,2,1,0:T(8,128)S(1)} %collective-permute-done.7, f32[2,2,16,1,512]{4,3,2,1,0:T(1,128)S(1)} %collective-permute-done.5, f32[1,2,16,8,512]{4,3,2,1,0:T(8,128)S(1)} %maximum_bitcast_fusion.1, f32[1,2,16,8,512]{4,3,2,1,0:T(8,128)S(1)} %maximum_bitcast_fusion, ...), kind=kLoop, calls=%fused_computation | loop fusion | flops 1644800 | bytes 2631680 | tf_op jit(solution)/shard_map/concatenate | solution.py:29
  62.1 0.8 add_multiply_fusion.3
  63.0 0.9 add_multiply_fusion.2
  63.9 0.8 multiply_bitcast_fusion.3
  64.7 0.9 multiply_bitcast_fusion.2
  65.9 2.1 %collective-permute-start.8 = (f32[2,2,16,1,512]{4,3,2,1,0:T(1,128)S(1)}, f32[2,2,16,1,512]{4,3,2,1,0:T(1,128)S(1)}, u32[]{:S(2)}, u32[]{:S(2)}) collective-permute-start(f32[2,2,16,1,512]{4,3,2,1,0:T(1,128)S(1)} %get-tuple-element.43), channel_id=1, source_target_pairs={{0,8},{8,16},{16,24},{24,0},{1,9},{9,17},{17,25},{25,1},{2,10},{10... | collective-permute-start | bytes 393224 | tf_op jit(solution)/shard_map/ppermute | solution.py:25
  68.0 1.8 %collective-permute-start.9 = (f32[2,2,16,1,512]{4,3,2,1,0:T(1,128)S(1)}, f32[2,2,16,1,512]{4,3,2,1,0:T(1,128)S(1)}, u32[]{:S(2)}, u32[]{:S(2)}) collective-permute-start(f32[2,2,16,1,512]{4,3,2,1,0:T(1,128)S(1)} %get-tuple-element.44), channel_id=1, source_target_pairs={{8,0},{16,8},{24,16},{0,24},{9,1},{17,9},{25,17},{1,25},{10,2},{18... | collective-permute-start | bytes 393224 | tf_op jit(solution)/shard_map/ppermute | solution.py:28
  69.8 4.4 %collective-permute-done.8 = f32[2,2,16,1,512]{4,3,2,1,0:T(1,128)S(1)} collective-permute-done((f32[2,2,16,1,512]{4,3,2,1,0:T(1,128)S(1)}, f32[2,2,16,1,512]{4,3,2,1,0:T(1,128)S(1)}, u32[]{:S(2)}, u32[]{:S(2)}) %collective-permute-start.8) | collective-permute-done | bytes 131104 | tf_op jit(solution)/shard_map/ppermute | solution.py:25
  74.2 1.9 %collective-permute-done.9 = f32[2,2,16,1,512]{4,3,2,1,0:T(1,128)S(1)} collective-permute-done((f32[2,2,16,1,512]{4,3,2,1,0:T(1,128)S(1)}, f32[2,2,16,1,512]{4,3,2,1,0:T(1,128)S(1)}, u32[]{:S(2)}, u32[]{:S(2)}) %collective-permute-start.9) | collective-permute-done | bytes 131104 | tf_op jit(solution)/shard_map/ppermute | solution.py:28
  76.5 2.6 %collective-permute-start.11 = (f32[2,2,16,10,1]{4,3,2,1,0:T(8,128)S(1)}, f32[2,2,16,10,1]{4,3,2,1,0:T(8,128)S(1)}, u32[]{:S(2)}, u32[]{:S(2)}) collective-permute-start(f32[2,2,16,10,1]{4,3,2,1,0:T(8,128)S(1)} %get-tuple-element.31), channel_id=1, source_target_pairs={{1,0},{2,1},{3,2},{4,3},{5,4},{6,5},{7,6},{0,7},{9,8},{10,9},{11,1... | collective-permute-start | bytes 7688 | tf_op jit(solution)/shard_map/ppermute | solution.py:28
  79.2 12.5 %collective-permute-done.10 = f32[2,2,16,10,1]{4,3,2,1,0:T(8,128)S(1)} collective-permute-done((f32[2,2,16,10,1]{4,3,2,1,0:T(8,128)S(1)}, f32[2,2,16,10,1]{4,3,2,1,0:T(8,128)S(1)}, u32[]{:S(2)}, u32[]{:S(2)}) %collective-permute-start.10) | collective-permute-done | bytes 2592 | tf_op jit(solution)/shard_map/ppermute | solution.py:25
  91.6 1.9 %pad_maximum_fusion.1 = f32[2,2,16,10,514]{4,3,2,1,0:T(8,128)S(1)} fusion(f32[2,2,16,10,1]{4,3,2,1,0:T(8,128)S(1)} %collective-permute-done.11, f32[2,2,16,1,512]{4,3,2,1,0:T(1,128)S(1)} %collective-permute-done.9, f32[1,2,16,8,512]{4,3,2,1,0:T(8,128)S(1)} %maximum_multiply_fusion.2, f32[1,2,16,8,512]{4,3,2,1,0:T(8,128)S(1)} %fusion.1, ...), kind=kLoop, calls=%fused_computation.1 | loop fusion | flops 1644800 | bytes 2631680 | tf_op jit(solution)/shard_map/concatenate | solution.py:29
  93.7 0.8 add_multiply_fusion.1
  94.6 0.9 add_multiply_fusion
  95.5 0.8 multiply_bitcast_fusion.1
  96.3 0.9 multiply_bitcast_fusion
  97.4 0.9 pad_maximum_fusion.20
  98.8 3.2 %collective-permute-start.13 = (f32[2,2,16,1,512]{4,3,2,1,0:T(1,128)}, f32[2,2,16,1,512]{4,3,2,1,0:T(1,128)}, u32[]{:S(2)}, u32[]{:S(2)}) collective-permute-start(f32[2,2,16,1,512]{4,3,2,1,0:T(1,128)} %get-tuple-element.42), channel_id=1, source_target_pairs={{8,0},{16,8},{24,16},{0,24},{9,1},{17,9},{25,17},{1,25},{10,2},{18... | collective-permute-start | bytes 393224 | tf_op jit(solution)/shard_map/ppermute | solution.py:28
  104.3 1.0 constant_dynamic-update-slice_fusion.1
  105.3 1.4 collective-permute-done.12
  107.0 2.1 %pad_maximum_fusion.7 = (f32[2,2,16,10,1]{4,3,2,1,0:T(8,128)}, f32[2,2,16,10,1]{4,3,2,1,0:T(8,128)}) fusion(f32[2,2,16,1,512]{4,3,2,1,0:T(1,128)} %collective-permute-done.13, f32[2,2,16,1,512]{4,3,2,1,0:T(1,128)} %collective-permute-done.12, f32[1,2,16,8,512]{4,3,2,1,0:T(8,128)S(1)} %fusion.5, f32[1,2,16,8,512]{4,3,2,1,0:T(8,128)S(1)} %fusion.4), kind=kLoop, calls=%fused_computation.23 | loop fusion | flops 3840 | bytes 1315840 | tf_op jit(solution)/shard_map/slice | solution.py:26
  109.1 2.6 %collective-permute-start.15 = (f32[2,2,16,10,1]{4,3,2,1,0:T(8,128)}, f32[2,2,16,10,1]{4,3,2,1,0:T(8,128)}, u32[]{:S(2)}, u32[]{:S(2)}) collective-permute-start(f32[2,2,16,10,1]{4,3,2,1,0:T(8,128)} %get-tuple-element.29), channel_id=1, source_target_pairs={{1,0},{2,1},{3,2},{4,3},{5,4},{6,5},{7,6},{0,7},{9,8},{10,9},{11,1... | collective-permute-start | bytes 7688 | tf_op jit(solution)/shard_map/ppermute | solution.py:28
  111.8 0.9 stack.146
  113.5 0.8 stack.156
  114.3 0.8 stack.157
  115.1 9.4 %collective-permute-done.14 = f32[2,2,16,10,1]{4,3,2,1,0:T(8,128)} collective-permute-done((f32[2,2,16,10,1]{4,3,2,1,0:T(8,128)}, f32[2,2,16,10,1]{4,3,2,1,0:T(8,128)}, u32[]{:S(2)}, u32[]{:S(2)}) %collective-permute-start.14) | collective-permute-done | bytes 2592 | tf_op jit(solution)/shard_map/ppermute | solution.py:25
  124.5 3.1 %pad_maximum_fusion.2 = f32[2,2,16,10,514]{4,3,2,1,0:T(8,128)S(1)} fusion(f32[2,2,16,10,1]{4,3,2,1,0:T(8,128)} %collective-permute-done.15, f32[2,2,16,1,512]{4,3,2,1,0:T(1,128)} %collective-permute-done.13, f32[1,2,16,8,512]{4,3,2,1,0:T(8,128)S(1)} %fusion.5, f32[1,2,16,8,512]{4,3,2,1,0:T(8,128)S(1)} %fusion.4, ...), kind=kLoop, calls=%fused_computation.2 | loop fusion | flops 1644800 | bytes 2631680 | tf_op jit(solution)/shard_map/concatenate | solution.py:29
  127.9 0.8 fusion.23
  128.7 0.8 stack.172
  129.5 2.4 %fusion.14 = f32[16,8,512]{2,1,0:T(8,128)} fusion(f32[16,10,514]{2,1,0:T(8,128)S(1)} %get-tuple-element.17, f32[16,10,514]{2,1,0:T(8,128)S(1)} %get-tuple-element.18, f32[16,10,514]{2,1,0:T(8,128)S(1)} %get-tuple-element.19, f32[8,512]{1,0:T(8,128)S(1)} %get-tuple-element.60, f32[8,512]{1,0:T(8,128)} %copy-done.5), kind=kLoop, calls=%fused_computation.58 | loop fusion | flops 1310720 | bytes 4489216 | tf_op jit(solution)/shard_map/mul | solution.py:65
  131.9 1.0 stack.173
  133.0 2.0 %fusion.38 = (f32[16]{0:T(128)S(1)}, f32[2,8,4,128]{3,2,1,0:T(4,128)S(1)}, f32[2,16,8,4,128]{4,3,2,1,0:T(4,128)S(1)}, f32[2,16,8,4,128]{4,3,2,1,0:T(4,128)S(1)}, f32[2,16,8,4,128]{4,3,2,1,0:T(4,128)S(1)}) fusion(f32[2,16,8,4,128]{4,3,2,1,0:T(4,128)S(1)} %copy-done.2, f32[2,16,8,4,128]{4,3,2,1,0:T(4,128)S(1)} %convolution_bitcast_fusion, ...), kind=kLoop, calls=%fused_computation.148 | loop fusion | flops 2088944 | bytes 4259904 | tf_op jit(solution)/shard_map/reduce_sum | solution.py:122
  135.7 10.6 %psum.14 = f32[4,16]{1,0:T(4,128)S(1)} all-reduce(f32[4,16]{1,0:T(4,128)S(1)} %pad_maximum_fusion.26), channel_id=1, replica_groups=mesh['gx'=4,'gy'=8] {'gx'}, use_global_device_ids=true, to_apply=%region_9.10 | all-reduce | flops 64 | bytes 512 | tf_op jit(solution)/shard_map/psum | solution.py:138
  146.2 11.8 %psum.15 = f32[4,16]{1,0:T(4,128)S(1)} all-reduce(f32[4,16]{1,0:T(4,128)S(1)} %psum.14), channel_id=1, replica_groups=mesh['gx'=4,'gy'=8] {'gy'}, use_global_device_ids=true, to_apply=%region_10.11 | all-reduce | flops 64 | bytes 512 | tf_op jit(solution)/shard_map/psum | solution.py:138
  (80 shorter events, 12.8 us)
Async XLA Ops:
  0.6 1.0 copy-start
  0.6 7.5 %copy-start.9 = (s32[32]{0:T(128)S(1)}, s32[32]{0:T(128)}, u32[]{:S(2)}) copy-start(s32[32]{0:T(128)} %param.7) | copy-start | bytes 388
  0.7 7.6 %copy-start.7 = (s32[2,8,512]{2,1,0:T(8,128)S(1)}, s32[2,8,512]{2,1,0:T(8,128)}, u32[]{:S(2)}) copy-start(s32[2,8,512]{2,1,0:T(8,128)} %param.6) | copy-start | bytes 98308
  2.0 20.5 %copy-start.8 = (f32[2,8,512]{2,1,0:T(8,128)S(1)}, f32[2,8,512]{2,1,0:T(8,128)}, u32[]{:S(2)}) copy-start(f32[2,8,512]{2,1,0:T(8,128)} %param.5) | copy-start | bytes 98308
  2.9 14.9 %all-to-all-start = ((bf16[8,2,16,8,128]{4,3,2,1,0:T(8,128)(2,1)}), bf16[8,2,16,8,128]{4,3,2,1,0:T(8,128)(2,1)S(1)}, u32[]{:S(2)}, u32[]{:S(2)}) async-start(bf16[8,2,16,8,128]{4,3,2,1,0:T(8,128)(2,1)} %copy.10), calls=%async_computation | async-start | bytes 1048576 | tf_op jit(solution)/shard_map/all_to_all | solution.py:90
  18.6 6.2 %collective-permute-start = (f32[1,2,16,1,512]{4,3,2,1,0:T(1,128)S(1)}, f32[1,2,16,1,512]{4,3,2,1,0:T(1,128)S(1)}, u32[]{:S(2)}, u32[]{:S(2)}) collective-permute-start(f32[1,2,16,1,512]{4,3,2,1,0:T(1,128)S(1)} %get-tuple-element.53), channel_id=1, source_target_pairs={{0,8},{8,16},{16,24},{24,0},{1,9},{9,17},{17,25},{25,1},{2,10},{10... | collective-permute-start | bytes 196616 | tf_op jit(solution)/shard_map/ppermute | solution.py:25
  20.3 5.0 %collective-permute-start.1 = (f32[1,2,16,1,512]{4,3,2,1,0:T(1,128)S(1)}, f32[1,2,16,1,512]{4,3,2,1,0:T(1,128)S(1)}, u32[]{:S(2)}, u32[]{:S(2)}) collective-permute-start(f32[1,2,16,1,512]{4,3,2,1,0:T(1,128)S(1)} %get-tuple-element.54), channel_id=1, source_target_pairs={{8,0},{16,8},{24,16},{0,24},{9,1},{17,9},{25,17},{1,25},{10,2},{18... | collective-permute-start | bytes 196616 | tf_op jit(solution)/shard_map/ppermute | solution.py:28
  22.5 73.8 %copy-start.5 = (f32[8,512]{1,0:T(8,128)}, f32[8,512]{1,0:T(8,128)S(1)}, u32[]{:S(2)}) copy-start(f32[8,512]{1,0:T(8,128)S(1)} %get-tuple-element.66) | copy-start | bytes 49156
  25.4 9.6 %collective-permute-start.2 = (f32[1,2,16,10,1]{4,3,2,1,0:T(8,128)S(1)}, f32[1,2,16,10,1]{4,3,2,1,0:T(8,128)S(1)}, u32[]{:S(2)}, u32[]{:S(2)}) collective-permute-start(f32[1,2,16,10,1]{4,3,2,1,0:T(8,128)S(1)} %get-tuple-element.47), channel_id=1, source_target_pairs={{0,1},{1,2},{2,3},{3,4},{4,5},{5,6},{6,7},{7,0},{8,9},{9,10},{10,1... | collective-permute-start | bytes 3848 | tf_op jit(solution)/shard_map/ppermute | solution.py:25
  25.5 9.5 %collective-permute-start.3 = (f32[1,2,16,10,1]{4,3,2,1,0:T(8,128)S(1)}, f32[1,2,16,10,1]{4,3,2,1,0:T(8,128)S(1)}, u32[]{:S(2)}, u32[]{:S(2)}) collective-permute-start(f32[1,2,16,10,1]{4,3,2,1,0:T(8,128)S(1)} %get-tuple-element.48), channel_id=1, source_target_pairs={{1,0},{2,1},{3,2},{4,3},{5,4},{6,5},{7,6},{0,7},{9,8},{10,9},{11,1... | collective-permute-start | bytes 3848 | tf_op jit(solution)/shard_map/ppermute | solution.py:28
  37.3 7.9 %collective-permute-start.4 = (f32[2,2,16,1,512]{4,3,2,1,0:T(1,128)S(1)}, f32[2,2,16,1,512]{4,3,2,1,0:T(1,128)S(1)}, u32[]{:S(2)}, u32[]{:S(2)}) collective-permute-start(f32[2,2,16,1,512]{4,3,2,1,0:T(1,128)S(1)} %get-tuple-element.45), channel_id=1, source_target_pairs={{0,8},{8,16},{16,24},{24,0},{1,9},{9,17},{17,25},{25,1},{2,10},{10... | collective-permute-start | bytes 393224 | tf_op jit(solution)/shard_map/ppermute | solution.py:25
  38.0 7.4 %collective-permute-start.5 = (f32[2,2,16,1,512]{4,3,2,1,0:T(1,128)S(1)}, f32[2,2,16,1,512]{4,3,2,1,0:T(1,128)S(1)}, u32[]{:S(2)}, u32[]{:S(2)}) collective-permute-start(f32[2,2,16,1,512]{4,3,2,1,0:T(1,128)S(1)} %get-tuple-element.46), channel_id=1, source_target_pairs={{8,0},{16,8},{24,16},{0,24},{9,1},{17,9},{25,17},{1,25},{10,2},{18... | collective-permute-start | bytes 393224 | tf_op jit(solution)/shard_map/ppermute | solution.py:28
  45.8 14.3 %collective-permute-start.6 = (f32[2,2,16,10,1]{4,3,2,1,0:T(8,128)S(1)}, f32[2,2,16,10,1]{4,3,2,1,0:T(8,128)S(1)}, u32[]{:S(2)}, u32[]{:S(2)}) collective-permute-start(f32[2,2,16,10,1]{4,3,2,1,0:T(8,128)S(1)} %get-tuple-element.32), channel_id=1, source_target_pairs={{0,1},{1,2},{2,3},{3,4},{4,5},{5,6},{6,7},{7,0},{8,9},{9,10},{10,1... | collective-permute-start | bytes 7688 | tf_op jit(solution)/shard_map/ppermute | solution.py:25
  45.8 14.2 %collective-permute-start.7 = (f32[2,2,16,10,1]{4,3,2,1,0:T(8,128)S(1)}, f32[2,2,16,10,1]{4,3,2,1,0:T(8,128)S(1)}, u32[]{:S(2)}, u32[]{:S(2)}) collective-permute-start(f32[2,2,16,10,1]{4,3,2,1,0:T(8,128)S(1)} %get-tuple-element.33), channel_id=1, source_target_pairs={{1,0},{2,1},{3,2},{4,3},{5,4},{6,5},{7,6},{0,7},{9,8},{10,9},{11,1... | collective-permute-start | bytes 7688 | tf_op jit(solution)/shard_map/ppermute | solution.py:28
  65.9 8.3 %collective-permute-start.8 = (f32[2,2,16,1,512]{4,3,2,1,0:T(1,128)S(1)}, f32[2,2,16,1,512]{4,3,2,1,0:T(1,128)S(1)}, u32[]{:S(2)}, u32[]{:S(2)}) collective-permute-start(f32[2,2,16,1,512]{4,3,2,1,0:T(1,128)S(1)} %get-tuple-element.43), channel_id=1, source_target_pairs={{0,8},{8,16},{16,24},{24,0},{1,9},{9,17},{17,25},{25,1},{2,10},{10... | collective-permute-start | bytes 393224 | tf_op jit(solution)/shard_map/ppermute | solution.py:25
  68.0 8.1 %collective-permute-start.9 = (f32[2,2,16,1,512]{4,3,2,1,0:T(1,128)S(1)}, f32[2,2,16,1,512]{4,3,2,1,0:T(1,128)S(1)}, u32[]{:S(2)}, u32[]{:S(2)}) collective-permute-start(f32[2,2,16,1,512]{4,3,2,1,0:T(1,128)S(1)} %get-tuple-element.44), channel_id=1, source_target_pairs={{8,0},{16,8},{24,16},{0,24},{9,1},{17,9},{25,17},{1,25},{10,2},{18... | collective-permute-start | bytes 393224 | tf_op jit(solution)/shard_map/ppermute | solution.py:28
  76.5 15.2 %collective-permute-start.10 = (f32[2,2,16,10,1]{4,3,2,1,0:T(8,128)S(1)}, f32[2,2,16,10,1]{4,3,2,1,0:T(8,128)S(1)}, u32[]{:S(2)}, u32[]{:S(2)}) collective-permute-start(f32[2,2,16,10,1]{4,3,2,1,0:T(8,128)S(1)} %get-tuple-element.30), channel_id=1, source_target_pairs={{0,1},{1,2},{2,3},{3,4},{4,5},{5,6},{6,7},{7,0},{8,9},{9,10},{10,1... | collective-permute-start | bytes 7688 | tf_op jit(solution)/shard_map/ppermute | solution.py:25
  76.5 15.1 %collective-permute-start.11 = (f32[2,2,16,10,1]{4,3,2,1,0:T(8,128)S(1)}, f32[2,2,16,10,1]{4,3,2,1,0:T(8,128)S(1)}, u32[]{:S(2)}, u32[]{:S(2)}) collective-permute-start(f32[2,2,16,10,1]{4,3,2,1,0:T(8,128)S(1)} %get-tuple-element.31), channel_id=1, source_target_pairs={{1,0},{2,1},{3,2},{4,3},{5,4},{6,5},{7,6},{0,7},{9,8},{10,9},{11,1... | collective-permute-start | bytes 7688 | tf_op jit(solution)/shard_map/ppermute | solution.py:28
  97.2 4.9 %copy-start.6 = (f32[2,8,4,128]{3,1,2,0:T(8,128)S(1)}, f32[2,8,4,128]{3,1,2,0:T(8,128)}, u32[]{:S(2)}) copy-start(f32[2,8,4,128]{3,1,2,0:T(8,128)} %get-tuple-element.55) | copy-start | bytes 98308
  98.3 8.5 %collective-permute-start.12 = (f32[2,2,16,1,512]{4,3,2,1,0:T(1,128)}, f32[2,2,16,1,512]{4,3,2,1,0:T(1,128)}, u32[]{:S(2)}, u32[]{:S(2)}) collective-permute-start(f32[2,2,16,1,512]{4,3,2,1,0:T(1,128)} %get-tuple-element.41), channel_id=1, source_target_pairs={{0,8},{8,16},{16,24},{24,0},{1,9},{9,17},{17,25},{25,1},{2,10},{10... | collective-permute-start | bytes 393224 | tf_op jit(solution)/shard_map/ppermute | solution.py:25
  98.8 8.1 %collective-permute-start.13 = (f32[2,2,16,1,512]{4,3,2,1,0:T(1,128)}, f32[2,2,16,1,512]{4,3,2,1,0:T(1,128)}, u32[]{:S(2)}, u32[]{:S(2)}) collective-permute-start(f32[2,2,16,1,512]{4,3,2,1,0:T(1,128)} %get-tuple-element.42), channel_id=1, source_target_pairs={{8,0},{16,8},{24,16},{0,24},{9,1},{17,9},{25,17},{1,25},{10,2},{18... | collective-permute-start | bytes 393224 | tf_op jit(solution)/shard_map/ppermute | solution.py:28
  104.3 7.5 %copy-start.4 = (f32[1,16,8,4,128]{4,3,2,1,0:T(4,128)S(1)}, f32[1,16,8,4,128]{4,3,2,1,0:T(4,128)}, u32[]{:S(2)}) copy-start(f32[1,16,8,4,128]{4,3,2,1,0:T(4,128)} %stack.135) | copy-start | bytes 786436
  109.1 15.4 %collective-permute-start.14 = (f32[2,2,16,10,1]{4,3,2,1,0:T(8,128)}, f32[2,2,16,10,1]{4,3,2,1,0:T(8,128)}, u32[]{:S(2)}, u32[]{:S(2)}) collective-permute-start(f32[2,2,16,10,1]{4,3,2,1,0:T(8,128)} %get-tuple-element.28), channel_id=1, source_target_pairs={{0,1},{1,2},{2,3},{3,4},{4,5},{5,6},{6,7},{7,0},{8,9},{9,10},{10,1... | collective-permute-start | bytes 7688 | tf_op jit(solution)/shard_map/ppermute | solution.py:25
  109.1 15.4 %collective-permute-start.15 = (f32[2,2,16,10,1]{4,3,2,1,0:T(8,128)}, f32[2,2,16,10,1]{4,3,2,1,0:T(8,128)}, u32[]{:S(2)}, u32[]{:S(2)}) collective-permute-start(f32[2,2,16,10,1]{4,3,2,1,0:T(8,128)} %get-tuple-element.29), channel_id=1, source_target_pairs={{1,0},{2,1},{3,2},{4,3},{5,4},{6,5},{7,6},{0,7},{9,8},{10,9},{11,1... | collective-permute-start | bytes 7688 | tf_op jit(solution)/shard_map/ppermute | solution.py:28
  111.8 12.7 %copy-start.1 = (f32[2,16,8,4,128]{4,3,2,1,0:T(4,128)}, f32[2,16,8,4,128]{4,3,2,1,0:T(4,128)S(1)}, u32[]{:S(2)}) copy-start(f32[2,16,8,4,128]{4,3,2,1,0:T(4,128)S(1)} %constant_dynamic-update-slice_fusion) | copy-start | bytes 1572868
  129.5 3.4 %copy-start.2 = (f32[2,16,8,4,128]{4,3,2,1,0:T(4,128)S(1)}, f32[2,16,8,4,128]{4,3,2,1,0:T(4,128)}, u32[]{:S(2)}) copy-start(f32[2,16,8,4,128]{4,3,2,1,0:T(4,128)} %copy-done.1) | copy-start | bytes 1572868
  129.5 3.4 %copy-start.3 = (f32[1,16,8,4,128]{4,3,2,1,0:T(4,128)S(1)}, f32[1,16,8,4,128]{4,3,2,1,0:T(4,128)}, u32[]{:S(2)}) copy-start(f32[1,16,8,4,128]{4,3,2,1,0:T(4,128)} %stack.146) | copy-start | bytes 786436
